TPU v7x, 32 devices: a whole 2x2x4 slice. The times are simulated.
32 devices in a mesh: blk: 8 (over z, x), rows: 4 (over y, core).
Axes of the slice: x: 2, y: 2, z: 4, core: 2. Of those that a mesh axis runs over, the one named last changes fastest.
Arguments:
- centers: int32 [512, 1], P(('blk', 'rows')), may hold values from 0 to 127, as said below
- gates_used: int32 [512], P(('blk', 'rows')), may hold values from 12 to 40
- jacobian: bfloat16 [512, 3, 40, 256], P(('blk', 'rows')), may hold values from -0.3984375 to 0.3984375
- weights: bfloat16 [512, 40], P(('blk', 'rows')), may hold values from 0.099609375 to 1
Outputs:
- hessian_band: float32 [128, 3, 256, 256], P(('blk', 'rows'))
Inputs may be any that keep to these rules, and one draw needn't show every extreme that they name: `centers`: cell block c is owned by blk index c // 16. Among the soundings of one device at most 4 are centred on blocks of one owner, and some owner gets exactly 4 of them; the number a device sends to the owner k places further along blk (cyclically) is the same for all devices of one rows index. Among the soundings of all devices of one rows index at most 2 share a centre block, and some block has exactly 2.
All inputs are finite; a program needn't handle non-finite values.
Results may differ from a plain program's by a relative error of at most 0.0024.
Values may be sent and summed in bfloat16 or wider, within the bound.
No kernel may reach another device: no remote copies, remote signals or barrier semaphores. Data moves between devices by JAX's collectives and lax.ppermute only.
A program may use at most 128 MiB of HBM per device.

v0:
```python
import jax
import jax.numpy as jnp
from jax import lax
from jax.sharding import PartitionSpec as P

KB = 16


def with_halo(block, sides, width):
    for axis, dim in sides:
        count = lax.axis_size(axis)
        forward = [(i, i + 1) for i in range(count - 1)]
        backward = [(target, source) for source, target in forward]
        low = lax.ppermute(
            lax.slice_in_dim(block, block.shape[dim] - width, None, axis=dim), axis, forward
        )
        high = lax.ppermute(lax.slice_in_dim(block, 0, width, axis=dim), axis, backward)
        block = jnp.concatenate([low, block, high], axis=dim)
    return block


def rank_among(labels):
    positions = jnp.arange(labels.shape[0], dtype=jnp.int32)
    before = (labels[None, :] == labels[:, None]) & (positions[None, :] < positions[:, None])
    return jnp.sum(before.astype(jnp.int32), axis=1)


def band_terms(buckets, bucket_wts, base, total_blocks):
    block_num, slot_len, foot_len, gate_len, cell_len = buckets.shape
    grid_pos = (
        base
        + jnp.arange(block_num, dtype=jnp.int32)[:, None]
        + jnp.arange(foot_len, dtype=jnp.int32)[None, :]
        - 1
    )
    inside = ((grid_pos >= 0) & (grid_pos < total_blocks)).astype(jnp.float32)
    scaled = (
        buckets.astype(jnp.float32)
        * bucket_wts.astype(jnp.float32)[:, :, None, :, None]
        * inside[:, None, :, None, None]
    ).astype(jnp.bfloat16)
    masked = buckets * inside.astype(jnp.bfloat16)[:, None, :, None, None]
    accum = jnp.zeros((block_num + 2, foot_len, cell_len, cell_len), jnp.float32)
    for lead_pos in range(foot_len):
        left = scaled[:, :, lead_pos].reshape(block_num, slot_len * gate_len, cell_len)
        for offset in range(foot_len - lead_pos):
            right = masked[:, :, lead_pos + offset].reshape(
                block_num, slot_len * gate_len, cell_len
            )
            term = lax.dot_general(
                left, right, (((1,), (1,)), ((0,), (0,))), preferred_element_type=jnp.float32
            )
            accum = accum.at[lead_pos : lead_pos + block_num, offset].add(term)
    return accum


def edge_rows(accum):
    return jnp.stack([accum[0], accum[accum.shape[0] - 1]])


def attach(accum, padded):
    block_num = accum.shape[0] - 2
    core = accum[1 : block_num + 1]
    core = core.at[0].add(padded[0])
    return core.at[block_num - 1].add(padded[3])


def on_device(centers, gates_used, jacobian, weights):
    blk_count = lax.axis_size("blk")
    sound_count, foot_len, gate_len, cell_len = jacobian.shape
    capacity = max(2, 2 * sound_count // blk_count)
    bucket_cap = max(2, 2 * sound_count // KB)
    slot_count = blk_count * capacity
    total_blocks = blk_count * KB
    centre_ids = centers[:, 0]
    owner = centre_ids // KB
    within = centre_ids - owner * KB
    order_in = rank_among(owner)
    gate_live = jnp.arange(gate_len, dtype=jnp.int32)[None, :] < gates_used[:, None]
    weight_live = jnp.where(gate_live, weights, jnp.zeros_like(weights))
    target = owner * capacity + order_in
    select = (target[None, :] == jnp.arange(slot_count, dtype=jnp.int32)[:, None]).astype(
        jnp.bfloat16
    )
    packed = (
        jnp.dot(select, jacobian.reshape(sound_count, -1), preferred_element_type=jnp.float32)
        .astype(jnp.bfloat16)
        .reshape(slot_count, foot_len, gate_len, cell_len)
    )
    packed_wts = jnp.dot(select, weight_live, preferred_element_type=jnp.float32).astype(
        jnp.bfloat16
    )
    packed_ids = jnp.dot(
        select, (within + 1).astype(jnp.bfloat16)[:, None], preferred_element_type=jnp.float32
    ).astype(jnp.bfloat16)[:, 0]
    received, received_wts, received_ids = (
        lax.all_to_all(packed, "blk", split_axis=0, concat_axis=0, tiled=True),
        lax.all_to_all(packed_wts, "blk", split_axis=0, concat_axis=0, tiled=True),
        lax.all_to_all(packed_ids, "blk", split_axis=0, concat_axis=0, tiled=True),
    )
    arrived_ids = received_ids.astype(jnp.int32)
    arrived_rank = rank_among(arrived_ids)
    bucket_target = jnp.where(arrived_ids > 0, (arrived_ids - 1) * bucket_cap + arrived_rank, -1)
    bucket_count = KB * bucket_cap
    bucket_sel = (
        bucket_target[None, :] == jnp.arange(bucket_count, dtype=jnp.int32)[:, None]
    ).astype(jnp.bfloat16)
    buckets = (
        jnp.dot(bucket_sel, received.reshape(slot_count, -1), preferred_element_type=jnp.float32)
        .astype(jnp.bfloat16)
        .reshape(KB, bucket_cap, foot_len, gate_len, cell_len)
    )
    bucket_wts = (
        jnp.dot(bucket_sel, received_wts, preferred_element_type=jnp.float32)
        .astype(jnp.bfloat16)
        .reshape(KB, bucket_cap, gate_len)
    )
    mine_blk = lax.axis_index("blk")
    share = KB // lax.axis_size("rows")
    moved, moved_wts = (
        lax.all_to_all(buckets, "rows", split_axis=0, concat_axis=1, tiled=True),
        lax.all_to_all(bucket_wts, "rows", split_axis=0, concat_axis=1, tiled=True),
    )
    base = mine_blk * KB + lax.axis_index("rows") * share
    accum = band_terms(moved, moved_wts, base, total_blocks)
    padded = with_halo(edge_rows(accum), ((("blk", "rows"), 0),), 1)
    return attach(accum, padded)


def solution(mesh):
    placed = (
        P(("blk", "rows"), None),
        P(("blk", "rows")),
        P(("blk", "rows"), None, None, None),
        P(("blk", "rows"), None),
    )
    return jax.shard_map(
        on_device,
        mesh=mesh,
        in_specs=placed,
        out_specs=P(("blk", "rows"), None, None, None),
        check_vma=False,
    )
```

profile of v0, /device:TPU:3, one launch (start us, length us, event | category | flops | bytes accessed | tf_op | source)
XLA Modules:
  0.0 140.4 jit_solution(17639520557241093231)
XLA Ops:
  2.2 0.8 fusion.9
  3.0 0.7 all_to_all.48
  3.6 5.8 %all-to-all-start = ((bf16[8,4,1]{1,2,0:T(2,128)(2,1)}), bf16[8,4,1]{1,2,0:T(2,128)(2,1)S(1)}, u32[]{:S(2)}, u32[]{:S(2)}) async-start(bf16[8,4,1]{1,2,0:T(2,128)(2,1)} %all_to_all.48), calls=%async_computation | async-start | bytes 8192 | tf_op jit(solution)/shard_map/all_to_all | solution.py:99
  9.4 1.5 %convolution_convert_fusion.3 = bf16[32,40]{1,0:T(8,128)(2,1)} fusion(s32[16]{0:T(128)S(1)} %multiply_add_fusion, bf16[16,40]{1,0:T(8,128)(2,1)} %param.23, s32[16]{0:T(128)} %param.21), kind=kOutput, calls=%fused_computation.21 | convolution fusion | flops 44032 | bytes 3968 | tf_op jit(solution)/shard_map/dot_general | solution.py:90
  10.9 1.4 copy.23
  12.3 1.2 all-to-all-done
  13.5 4.4 %all-to-all-start.3 = ((bf16[8,4,40]{2,1,0:T(4,128)(2,1)}), bf16[8,4,40]{2,1,0:T(4,128)(2,1)S(1)}, u32[]{:S(2)}, u32[]{:S(2)}) async-start(bf16[8,4,40]{2,1,0:T(4,128)(2,1)} %bitcast.7), calls=%async_computation.3 | async-start | bytes 16384 | tf_op jit(solution)/shard_map/all_to_all | solution.py:98
  18.6 1.7 %copy.24 = bf16[4,8,120,256]{3,2,1,0:T(8,128)(2,1)} copy(bf16[4,8,120,256]{3,1,2,0:T(8,128)(2,1)S(1)} %bitcast.109) | data formatting | bytes 3932160
  20.2 1.9 %all-to-all-done.3 = bf16[8,4,40]{2,1,0:T(4,128)(2,1)S(1)} async-done(((bf16[8,4,40]{2,1,0:T(4,128)(2,1)}), bf16[8,4,40]{2,1,0:T(4,128)(2,1)S(1)}, u32[]{:S(2)}, u32[]{:S(2)}) %all-to-all-start.3) | async-done | bytes 2592 | tf_op jit(solution)/shard_map/all_to_all | solution.py:98
  22.1 4.7 %all-to-all-start.1 = ((bf16[32,3,40,256]{3,2,1,0:T(8,128)(2,1)}), bf16[32,3,40,256]{3,2,1,0:T(8,128)(2,1)S(1)}, u32[]{:S(2)}, u32[]{:S(2)}) async-start(bf16[32,3,40,256]{3,2,1,0:T(8,128)(2,1)} %bitcast.108), calls=%async_computation.1 | async-start | bytes 3932160 | tf_op jit(solution)/shard_map/all_to_all | solution.py:97
  27.2 0.7 reshape.492
  27.9 43.5 %all-to-all-done.1 = bf16[32,3,40,256]{3,2,1,0:T(8,128)(2,1)S(1)} async-done(((bf16[32,3,40,256]{3,2,1,0:T(8,128)(2,1)}), bf16[32,3,40,256]{3,2,1,0:T(8,128)(2,1)S(1)}, u32[]{:S(2)}, u32[]{:S(2)}) %all-to-all-start.1) | async-done | bytes 1966112 | tf_op jit(solution)/shard_map/all_to_all | solution.py:97
  71.5 4.7 %all-to-all-start.4 = ((bf16[4,2,160]{2,1,0:T(2,128)(2,1)}), bf16[4,2,160]{2,1,0:T(2,128)(2,1)S(1)}, u32[]{:S(2)}, u32[]{:S(2)}) async-start(bf16[4,2,160]{2,1,0:T(2,128)(2,1)} %reshape.492), calls=%async_computation.4 | async-start | bytes 8192 | tf_op jit(solution)/shard_map/all_to_all | solution.py:122
  77.2 1.7 %copy.26 = bf16[4,8,120,256]{3,2,1,0:T(8,128)(2,1)} copy(bf16[4,8,120,256]{3,1,2,0:T(8,128)(2,1)S(1)} %bitcast.111) | data formatting | bytes 3932160
  79.2 4.3 %all-to-all-start.2 = ((bf16[16,2,3,40,256]{4,3,2,1,0:T(8,128)(2,1)}), bf16[16,2,3,40,256]{4,3,2,1,0:T(8,128)(2,1)S(1)}, u32[]{:S(2)}, u32[]{:S(2)}) async-start(bf16[16,2,3,40,256]{4,3,2,1,0:T(8,128)(2,1)} %bitcast.42), calls=%async_computation.2 | async-start | bytes 3932160 | tf_op jit(solution)/shard_map/all_to_all | solution.py:121
  84.7 0.8 and_reduce_fusion
  85.6 21.2 %all-to-all-done.2 = bf16[16,2,3,40,256]{4,3,2,1,0:T(8,128)(2,1)S(1)} async-done(((bf16[16,2,3,40,256]{4,3,2,1,0:T(8,128)(2,1)}), bf16[16,2,3,40,256]{4,3,2,1,0:T(8,128)(2,1)S(1)}, u32[]{:S(2)}, u32[]{:S(2)}) %all-to-all-start.2) | async-done | bytes 1966112 | tf_op jit(solution)/shard_map/all_to_all | solution.py:121
  109.0 1.7 %fusion.1 = f32[6,3,256,256]{3,2,0,1:T(8,128)S(1)} fusion(f32[6,3,256,256]{3,2,0,1:T(8,128)S(1)} %scatter-add.26, s32[]{:T(128)} %bitcast.16, s32[]{:T(128)} %bitcast.17, bf16[4,320,256]{2,1,0:T(8,128)(2,1)S(1)} %bitcast.101, bf16[4,320,256]{2,1,0:T(8,128)(2,1)S(1)} %bitcast.114, f32[4,1,256,256]{3,2,0,1:T(8,128)S(1)} %convolution_bitcast_fusion.5), kind=kOutput, calls=%fused_computation.12 | convolution fusion | flops 168034304 | bytes 3407880 | tf_op jit(solution)/shard_map/dot_general | solution.py:50
  110.7 2.4 %fusion.8 = f32[6,3,256,256]{3,2,0,1:T(8,128)S(1)} fusion(f32[6,3,256,256]{3,2,0,1:T(8,128)S(1)} %fusion.1, s32[]{:T(128)} %bitcast.20, s32[]{:T(128)} %bitcast.21, bf16[4,320,256]{2,1,0:T(8,128)(2,1)S(1)} %bitcast.102, bf16[4,320,256]{2,1,0:T(8,128)(2,1)S(1)} %bitcast.103, pred[]{:T(512)} %and_reduce_fusion), kind=kOutput, calls=%fused_computation.19 | convolution fusion | flops 168296448 | bytes 3407881 | tf_op jit(solution)/shard_map/dot_general | solution.py:50
  115.2 2.9 %collective-permute-start = (f32[1,3,256,256]{3,2,0,1:T(8,128)S(1)}, f32[1,3,256,256]{3,2,0,1:T(8,128)S(1)}, u32[]{:S(2)}, u32[]{:S(2)}) collective-permute-start(f32[1,3,256,256]{3,2,0,1:T(8,128)S(1)} %get-tuple-element.102), channel_id=1, source_target_pairs={{0,1},{1,2},{2,3},{3,4},{4,5},{5,6},{6,7},{7,8},{8,9},{9,10},{10,1... | collective-permute-start | bytes 2359304 | tf_op jit(solution)/shard_map/ppermute | solution.py:14
  118.1 1.9 %collective-permute-start.1 = (f32[1,3,256,256]{3,2,0,1:T(8,128)S(1)}, f32[1,3,256,256]{3,2,0,1:T(8,128)S(1)}, u32[]{:S(2)}, u32[]{:S(2)}) collective-permute-start(f32[1,3,256,256]{3,2,0,1:T(8,128)S(1)} %get-tuple-element.101), channel_id=1, source_target_pairs={{1,0},{2,1},{3,2},{4,3},{5,4},{6,5},{7,6},{8,7},{9,8},{10,9},{11,1... | collective-permute-start | bytes 2359304 | tf_op jit(solution)/shard_map/ppermute | solution.py:17
  120.3 15.2 %collective-permute-done = f32[1,3,256,256]{3,2,0,1:T(8,128)S(1)} collective-permute-done((f32[1,3,256,256]{3,2,0,1:T(8,128)S(1)}, f32[1,3,256,256]{3,2,0,1:T(8,128)S(1)}, u32[]{:S(2)}, u32[]{:S(2)}) %collective-permute-start) | collective-permute-done | bytes 786464 | tf_op jit(solution)/shard_map/ppermute | solution.py:14
  135.6 2.6 %collective-permute-done.1 = f32[1,3,256,256]{3,2,0,1:T(8,128)S(1)} collective-permute-done((f32[1,3,256,256]{3,2,0,1:T(8,128)S(1)}, f32[1,3,256,256]{3,2,0,1:T(8,128)S(1)}, u32[]{:S(2)}, u32[]{:S(2)}) %collective-permute-start.1) | collective-permute-done | bytes 786464 | tf_op jit(solution)/shard_map/ppermute | solution.py:17
  138.3 2.1 %copy.22 = f32[4,3,256,256]{3,2,1,0:T(8,128)} copy(f32[4,3,256,256]{3,2,0,1:T(8,128)S(1)} %fusion.10) | data formatting | bytes 6291456 | tf_op jit(solution)/shard_map/scatter-add | solution.py:65
  (39 shorter events, 10.7 us)
Async XLA Ops:
  3.6 9.9 %all-to-all-start = ((bf16[8,4,1]{1,2,0:T(2,128)(2,1)}), bf16[8,4,1]{1,2,0:T(2,128)(2,1)S(1)}, u32[]{:S(2)}, u32[]{:S(2)}) async-start(bf16[8,4,1]{1,2,0:T(2,128)(2,1)} %all_to_all.48), calls=%async_computation | async-start | bytes 8192 | tf_op jit(solution)/shard_map/all_to_all | solution.py:99
  13.5 8.6 %all-to-all-start.3 = ((bf16[8,4,40]{2,1,0:T(4,128)(2,1)}), bf16[8,4,40]{2,1,0:T(4,128)(2,1)S(1)}, u32[]{:S(2)}, u32[]{:S(2)}) async-start(bf16[8,4,40]{2,1,0:T(4,128)(2,1)} %bitcast.7), calls=%async_computation.3 | async-start | bytes 16384 | tf_op jit(solution)/shard_map/all_to_all | solution.py:98
  22.1 49.3 %all-to-all-start.1 = ((bf16[32,3,40,256]{3,2,1,0:T(8,128)(2,1)}), bf16[32,3,40,256]{3,2,1,0:T(8,128)(2,1)S(1)}, u32[]{:S(2)}, u32[]{:S(2)}) async-start(bf16[32,3,40,256]{3,2,1,0:T(8,128)(2,1)} %bitcast.108), calls=%async_computation.1 | async-start | bytes 3932160 | tf_op jit(solution)/shard_map/all_to_all | solution.py:97
  71.5 7.8 %all-to-all-start.4 = ((bf16[4,2,160]{2,1,0:T(2,128)(2,1)}), bf16[4,2,160]{2,1,0:T(2,128)(2,1)S(1)}, u32[]{:S(2)}, u32[]{:S(2)}) async-start(bf16[4,2,160]{2,1,0:T(2,128)(2,1)} %reshape.492), calls=%async_computation.4 | async-start | bytes 8192 | tf_op jit(solution)/shard_map/all_to_all | solution.py:122
  77.2 7.5 %copy-start = (s32[4]{0:T(128)S(1)}, s32[4]{0:T(128)}, u32[]{:S(2)}) copy-start(s32[4]{0:T(128)} %constant.269.clone.1) | copy-start | bytes 52
  79.2 27.6 %all-to-all-start.2 = ((bf16[16,2,3,40,256]{4,3,2,1,0:T(8,128)(2,1)}), bf16[16,2,3,40,256]{4,3,2,1,0:T(8,128)(2,1)S(1)}, u32[]{:S(2)}, u32[]{:S(2)}) async-start(bf16[16,2,3,40,256]{4,3,2,1,0:T(8,128)(2,1)} %bitcast.42), calls=%async_computation.2 | async-start | bytes 3932160 | tf_op jit(solution)/shard_map/all_to_all | solution.py:121
  115.2 20.2 %collective-permute-start = (f32[1,3,256,256]{3,2,0,1:T(8,128)S(1)}, f32[1,3,256,256]{3,2,0,1:T(8,128)S(1)}, u32[]{:S(2)}, u32[]{:S(2)}) collective-permute-start(f32[1,3,256,256]{3,2,0,1:T(8,128)S(1)} %get-tuple-element.102), channel_id=1, source_target_pairs={{0,1},{1,2},{2,3},{3,4},{4,5},{5,6},{6,7},{7,8},{8,9},{9,10},{10,1... | collective-permute-start | bytes 2359304 | tf_op jit(solution)/shard_map/ppermute | solution.py:14
  118.1 20.0 %collective-permute-start.1 = (f32[1,3,256,256]{3,2,0,1:T(8,128)S(1)}, f32[1,3,256,256]{3,2,0,1:T(8,128)S(1)}, u32[]{:S(2)}, u32[]{:S(2)}) collective-permute-start(f32[1,3,256,256]{3,2,0,1:T(8,128)S(1)} %get-tuple-element.101), channel_id=1, source_target_pairs={{1,0},{2,1},{3,2},{4,3},{5,4},{6,5},{7,6},{8,7},{9,8},{10,9},{11,1... | collective-permute-start | bytes 2359304 | tf_op jit(solution)/shard_map/ppermute | solution.py:17
where the time goes:
time: 141 us; the launch traced here: 140 us
  waiting for transfers between devices  86 us (61%)
  starting transfers between devices  28.6 us (20%)
  local copies, waits for them, and re-layouts  11.3 us (8%)
  matrix products  10.2 us (7%)
  other arithmetic  4.17 us (3%)
    all_to_all x1, waiting for transfers between devices, on_device(): lax.all_to_all(packed, 'blk', split_axis=0, concat_axis=0, tiled=True)  43.5 us
    all_to_all x1, waiting for transfers between devices, on_device(): lax.all_to_all(buckets, 'rows', split_axis=0, concat_axis=1, tiled=True)  21.2 us
    ppermute x1, waiting for transfers between devices, with_halo(): lax.ppermute(lax.slice_in_dim(block, block.shape[dim] - width, None, axis...  15.2 us
    dot_general x6, matrix products, band_terms(): lax.dot_general(left, right, (((1,), (1,)), ((0,), (0,))), preferred_elem...  6.5 us
    unnamed x8, local copies, waits for them, and re-layouts  5.87 us
    all_to_all x1, starting transfers between devices, on_device(): lax.all_to_all(packed_ids, 'blk', split_axis=0, concat_axis=0, tiled=True)  5.78 us
    all_to_all x1, starting transfers between devices, on_device(): lax.all_to_all(packed, 'blk', split_axis=0, concat_axis=0, tiled=True)  4.71 us
    all_to_all x1, starting transfers between devices, on_device(): lax.all_to_all(bucket_wts, 'rows', split_axis=0, concat_axis=1, tiled=True)  4.67 us
  transfers between devices with their start and end apart: 7, of which 7 were waited for; matrix products, arithmetic and copies ran while one was open for 8% of the time, Pallas kernels for 0%

commit v1 on v0

--- a/solution.py
+++ b/solution.py
@@ -4,6 +4,22 @@
 from jax.sharding import PartitionSpec as P
 
 KB = 16
+
+
+def pairwise_exchange(x, axis, split, join):
+    ways, here = (lax.axis_size(axis), lax.axis_index(axis))
+    width = x.shape[split] // ways
+    dims = list(x.shape)
+    dims[split] = width
+    height = dims[join]
+    dims[join] = height * ways
+    full = jnp.zeros(dims, x.dtype)
+    for mask in range(ways):
+        part = lax.dynamic_slice_in_dim(x, (here ^ mask) * width, width, axis=split)
+        if mask:
+            part = lax.ppermute(part, axis, [(d, d ^ mask) for d in range(ways)])
+        full = lax.dynamic_update_slice_in_dim(full, part, (here ^ mask) * height, axis=join)
+    return full
 
 
 def with_halo(block, sides, width):
@@ -118,7 +134,7 @@
     mine_blk = lax.axis_index("blk")
     share = KB // lax.axis_size("rows")
     moved, moved_wts = (
-        lax.all_to_all(buckets, "rows", split_axis=0, concat_axis=1, tiled=True),
+        pairwise_exchange(buckets, "rows", 0, 1),
         lax.all_to_all(bucket_wts, "rows", split_axis=0, concat_axis=1, tiled=True),
     )
     base = mine_blk * KB + lax.axis_index("rows") * share

time: 141 us -> 135 us (0.957)
  waiting for transfers between devices: 86 us -> 83.3 us
  starting transfers between devices: 28.6 us -> 26.8 us
    all_to_all x1 -> x0, waiting for transfers between devices: 21.2 us -> none  [on_device(): lax.all_to_all(buckets, 'rows', split_axis=0, concat_axis=1, tiled=True)]
    ppermute x0 -> x3, waiting for transfers between devices: none -> 20.8 us  [pairwise_exchange(): part = lax.ppermute(part, axis, [(d, d ^ mask) for d in range(ways)])]
    all_to_all x1 -> x0, starting transfers between devices: 4.27 us -> none  [on_device(): lax.all_to_all(buckets, 'rows', split_axis=0, concat_axis=1, tiled=True)]
    ppermute x0 -> x3, starting transfers between devices: none -> 2.51 us  [pairwise_exchange(): part = lax.ppermute(part, axis, [(d, d ^ mask) for d in range(ways)])]
  transfers between devices with their start and end apart: 7 -> 9, of which waited for: 7 -> 8; matrix products, arithmetic and copies ran while one was open for 8% -> 8% of each run, Pallas kernels for 0% -> 0%
where the time goes in v1:
time: 135 us
  waiting for transfers between devices  83.3 us (62%)
  starting transfers between devices  26.8 us (20%)
  local copies, waits for them, and re-layouts  10.3 us (8%)
  matrix products  10.1 us (7%)
  other arithmetic  4.13 us (3%)
    all_to_all x1, waiting for transfers between devices, on_device(): lax.all_to_all(packed, 'blk', split_axis=0, concat_axis=0, tiled=True)  42.2 us
    ppermute x3, waiting for transfers between devices, pairwise_exchange(): part = lax.ppermute(part, axis, [(d, d ^ mask) for d in range(ways)])  20.8 us
    ppermute x1, waiting for transfers between devices, with_halo(): lax.ppermute(lax.slice_in_dim(block, block.shape[dim] - width, None, axis...  15.2 us
    dot_general x6, matrix products, band_terms(): lax.dot_general(left, right, (((1,), (1,)), ((0,), (0,))), preferred_elem...  6.48 us
    all_to_all x1, starting transfers between devices, on_device(): lax.all_to_all(packed_ids, 'blk', split_axis=0, concat_axis=0, tiled=True)  5.78 us
    all_to_all x1, starting transfers between devices, on_device(): lax.all_to_all(packed, 'blk', split_axis=0, concat_axis=0, tiled=True)  4.71 us
    all_to_all x1, starting transfers between devices, on_device(): lax.all_to_all(bucket_wts, 'rows', split_axis=0, concat_axis=1, tiled=True)  4.67 us
    unnamed x8, local copies, waits for them, and re-layouts  4.6 us
  transfers between devices with their start and end apart: 9, of which 8 were waited for; matrix products, arithmetic and copies ran while one was open for 8% of the time, Pallas kernels for 0%

profile of v1, /device:TPU:3, one launch (start us, length us, event | category | flops | bytes accessed | tf_op | source)
XLA Modules:
  0.0 134.9 jit_solution(18354022045185620302)
XLA Ops:
  2.2 0.8 fusion.9
  3.6 5.8 %all-to-all-start = ((bf16[8,4,1]{1,2,0:T(2,128)(2,1)}), bf16[8,4,1]{1,2,0:T(2,128)(2,1)S(1)}, u32[]{:S(2)}, u32[]{:S(2)}) async-start(bf16[8,4,1]{1,2,0:T(2,128)(2,1)} %all_to_all.31), calls=%async_computation | async-start | bytes 8192 | tf_op jit(solution)/shard_map/all_to_all | solution.py:115
  9.4 1.5 %convolution_convert_fusion.3 = bf16[32,40]{1,0:T(8,128)(2,1)} fusion(s32[16]{0:T(128)S(1)} %multiply_add_fusion, bf16[16,40]{1,0:T(8,128)(2,1)} %param.23, s32[16]{0:T(128)} %param.21), kind=kOutput, calls=%fused_computation.21 | convolution fusion | flops 44032 | bytes 3968 | tf_op jit(solution)/shard_map/dot_general | solution.py:106
  10.9 1.4 %copy.38 = bf16[2,8,120,256]{3,1,2,0:T(8,128)(2,1)S(1)} copy(bf16[2,8,120,256]{3,2,1,0:T(8,128)(2,1)} %bitcast.113) | data formatting | bytes 1966080
  12.3 1.2 all-to-all-done
  13.5 4.4 %all-to-all-start.2 = ((bf16[8,4,40]{2,1,0:T(4,128)(2,1)}), bf16[8,4,40]{2,1,0:T(4,128)(2,1)S(1)}, u32[]{:S(2)}, u32[]{:S(2)}) async-start(bf16[8,4,40]{2,1,0:T(4,128)(2,1)} %bitcast.4), calls=%async_computation.2 | async-start | bytes 16384 | tf_op jit(solution)/shard_map/all_to_all | solution.py:114
  18.6 1.7 %copy.39 = bf16[4,8,120,256]{3,2,1,0:T(8,128)(2,1)} copy(bf16[4,8,120,256]{3,1,2,0:T(8,128)(2,1)S(1)} %bitcast.103) | data formatting | bytes 3932160
  20.2 1.9 %all-to-all-done.2 = bf16[8,4,40]{2,1,0:T(4,128)(2,1)S(1)} async-done(((bf16[8,4,40]{2,1,0:T(4,128)(2,1)}), bf16[8,4,40]{2,1,0:T(4,128)(2,1)S(1)}, u32[]{:S(2)}, u32[]{:S(2)}) %all-to-all-start.2) | async-done | bytes 2592 | tf_op jit(solution)/shard_map/all_to_all | solution.py:114
  22.1 4.7 %all-to-all-start.1 = ((bf16[32,3,40,256]{3,2,1,0:T(8,128)(2,1)}), bf16[32,3,40,256]{3,2,1,0:T(8,128)(2,1)S(1)}, u32[]{:S(2)}, u32[]{:S(2)}) async-start(bf16[32,3,40,256]{3,2,1,0:T(8,128)(2,1)} %bitcast.102), calls=%async_computation.1 | async-start | bytes 3932160 | tf_op jit(solution)/shard_map/all_to_all | solution.py:113
  27.4 0.7 and_reduce_fusion
  29.3 42.2 %all-to-all-done.1 = bf16[32,3,40,256]{3,2,1,0:T(8,128)(2,1)S(1)} async-done(((bf16[32,3,40,256]{3,2,1,0:T(8,128)(2,1)}), bf16[32,3,40,256]{3,2,1,0:T(8,128)(2,1)S(1)}, u32[]{:S(2)}, u32[]{:S(2)}) %all-to-all-start.1) | async-done | bytes 1966112 | tf_op jit(solution)/shard_map/all_to_all | solution.py:113
  71.5 4.7 %all-to-all-start.3 = ((bf16[4,2,160]{2,1,0:T(2,128)(2,1)}), bf16[4,2,160]{2,1,0:T(2,128)(2,1)S(1)}, u32[]{:S(2)}, u32[]{:S(2)}) async-start(bf16[4,2,160]{2,1,0:T(2,128)(2,1)} %reshape.492), calls=%async_computation.3 | async-start | bytes 8192 | tf_op jit(solution)/shard_map/all_to_all | solution.py:138
  78.4 0.8 all-to-all-done.3
  79.3 1.0 collective-permute-start.1
  80.3 1.4 %collective-permute-start.2 = (bf16[4,2,3,40,256]{4,3,2,1,0:T(8,128)(2,1)S(1)}, bf16[4,2,3,40,256]{4,3,2,1,0:T(8,128)(2,1)S(1)}, u32[]{:S(2)}, u32[]{:S(2)}) collective-permute-start(bf16[4,2,3,40,256]{4,3,2,1,0:T(8,128)(2,1)S(1)} %get-tuple-element.109), channel_id=1, source_target_pairs={{0,3},{1,2},{2,1},{3,0},{4,7},{5,6},{6,5},{7,4},{8,11},{9,10},{10,... | collective-permute-start | bytes 1474568 | tf_op jit(solution)/shard_map/ppermute | solution.py:20
  82.0 9.4 %collective-permute-done.1 = bf16[4,2,3,40,256]{4,3,2,1,0:T(8,128)(2,1)S(1)} collective-permute-done((bf16[4,2,3,40,256]{4,3,2,1,0:T(8,128)(2,1)S(1)}, bf16[4,2,3,40,256]{4,3,2,1,0:T(8,128)(2,1)S(1)}, u32[]{:S(2)}, u32[]{:S(2)}) %collective-permute-start.1) | collective-permute-done | bytes 491552 | tf_op jit(solution)/shard_map/ppermute | solution.py:20
  91.5 11.3 %collective-permute-done.2 = bf16[4,2,3,40,256]{4,3,2,1,0:T(8,128)(2,1)S(1)} collective-permute-done((bf16[4,2,3,40,256]{4,3,2,1,0:T(8,128)(2,1)S(1)}, bf16[4,2,3,40,256]{4,3,2,1,0:T(8,128)(2,1)S(1)}, u32[]{:S(2)}, u32[]{:S(2)}) %collective-permute-start.2) | collective-permute-done | bytes 491552 | tf_op jit(solution)/shard_map/ppermute | solution.py:20
  105.0 1.7 %fusion.1 = f32[6,3,256,256]{3,2,0,1:T(8,128)S(1)} fusion(f32[6,3,256,256]{3,2,0,1:T(8,128)S(1)} %scatter-add.26, s32[]{:T(128)} %bitcast.13, s32[]{:T(128)} %bitcast.14, bf16[4,320,256]{2,1,0:T(8,128)(2,1)S(1)} %bitcast.95, bf16[4,320,256]{2,1,0:T(8,128)(2,1)S(1)} %bitcast.108, f32[4,1,256,256]{3,2,0,1:T(8,128)S(1)} %convolution_bitcast_fusion.5), kind=kOutput, calls=%fused_computation.12 | convolution fusion | flops 168034304 | bytes 3407880 | tf_op jit(solution)/shard_map/dot_general | solution.py:66
  106.7 2.4 %fusion.8 = f32[6,3,256,256]{3,2,0,1:T(8,128)S(1)} fusion(f32[6,3,256,256]{3,2,0,1:T(8,128)S(1)} %fusion.1, s32[]{:T(128)} %bitcast.17, s32[]{:T(128)} %bitcast.18, bf16[4,320,256]{2,1,0:T(8,128)(2,1)S(1)} %bitcast.96, bf16[4,320,256]{2,1,0:T(8,128)(2,1)S(1)} %bitcast.97, pred[]{:T(512)} %and_reduce_fusion), kind=kOutput, calls=%fused_computation.19 | convolution fusion | flops 168296448 | bytes 3407881 | tf_op jit(solution)/shard_map/dot_general | solution.py:66
  111.2 2.8 %collective-permute-start.3 = (f32[1,3,256,256]{3,2,0,1:T(8,128)S(1)}, f32[1,3,256,256]{3,2,0,1:T(8,128)S(1)}, u32[]{:S(2)}, u32[]{:S(2)}) collective-permute-start(f32[1,3,256,256]{3,2,0,1:T(8,128)S(1)} %get-tuple-element.102), channel_id=1, source_target_pairs={{0,1},{1,2},{2,3},{3,4},{4,5},{5,6},{6,7},{7,8},{8,9},{9,10},{10,1... | collective-permute-start | bytes 2359304 | tf_op jit(solution)/shard_map/ppermute | solution.py:30
  114.0 1.9 %collective-permute-start.4 = (f32[1,3,256,256]{3,2,0,1:T(8,128)S(1)}, f32[1,3,256,256]{3,2,0,1:T(8,128)S(1)}, u32[]{:S(2)}, u32[]{:S(2)}) collective-permute-start(f32[1,3,256,256]{3,2,0,1:T(8,128)S(1)} %get-tuple-element.101), channel_id=1, source_target_pairs={{1,0},{2,1},{3,2},{4,3},{5,4},{6,5},{7,6},{8,7},{9,8},{10,9},{11,1... | collective-permute-start | bytes 2359304 | tf_op jit(solution)/shard_map/ppermute | solution.py:33
  116.1 15.2 %collective-permute-done.3 = f32[1,3,256,256]{3,2,0,1:T(8,128)S(1)} collective-permute-done((f32[1,3,256,256]{3,2,0,1:T(8,128)S(1)}, f32[1,3,256,256]{3,2,0,1:T(8,128)S(1)}, u32[]{:S(2)}, u32[]{:S(2)}) %collective-permute-start.3) | collective-permute-done | bytes 786464 | tf_op jit(solution)/shard_map/ppermute | solution.py:30
  131.4 1.2 collective-permute-done.4
  132.8 2.1 %copy.37 = f32[4,3,256,256]{3,2,1,0:T(8,128)} copy(f32[4,3,256,256]{3,2,0,1:T(8,128)S(1)} %fusion.10) | data formatting | bytes 6291456 | tf_op jit(solution)/shard_map/scatter-add | solution.py:81
  (48 shorter events, 12.5 us)
Async XLA Ops:
  3.6 9.9 %all-to-all-start = ((bf16[8,4,1]{1,2,0:T(2,128)(2,1)}), bf16[8,4,1]{1,2,0:T(2,128)(2,1)S(1)}, u32[]{:S(2)}, u32[]{:S(2)}) async-start(bf16[8,4,1]{1,2,0:T(2,128)(2,1)} %all_to_all.31), calls=%async_computation | async-start | bytes 8192 | tf_op jit(solution)/shard_map/all_to_all | solution.py:115
  13.5 8.6 %all-to-all-start.2 = ((bf16[8,4,40]{2,1,0:T(4,128)(2,1)}), bf16[8,4,40]{2,1,0:T(4,128)(2,1)S(1)}, u32[]{:S(2)}, u32[]{:S(2)}) async-start(bf16[8,4,40]{2,1,0:T(4,128)(2,1)} %bitcast.4), calls=%async_computation.2 | async-start | bytes 16384 | tf_op jit(solution)/shard_map/all_to_all | solution.py:114
  18.6 8.9 %copy-start = (s32[4]{0:T(128)S(1)}, s32[4]{0:T(128)}, u32[]{:S(2)}) copy-start(s32[4]{0:T(128)} %constant.276.clone.1) | copy-start | bytes 52
  22.1 49.3 %all-to-all-start.1 = ((bf16[32,3,40,256]{3,2,1,0:T(8,128)(2,1)}), bf16[32,3,40,256]{3,2,1,0:T(8,128)(2,1)S(1)}, u32[]{:S(2)}, u32[]{:S(2)}) async-start(bf16[32,3,40,256]{3,2,1,0:T(8,128)(2,1)} %bitcast.102), calls=%async_computation.1 | async-start | bytes 3932160 | tf_op jit(solution)/shard_map/all_to_all | solution.py:113
  71.5 7.8 %all-to-all-start.3 = ((bf16[4,2,160]{2,1,0:T(2,128)(2,1)}), bf16[4,2,160]{2,1,0:T(2,128)(2,1)S(1)}, u32[]{:S(2)}, u32[]{:S(2)}) async-start(bf16[4,2,160]{2,1,0:T(2,128)(2,1)} %reshape.492), calls=%async_computation.3 | async-start | bytes 8192 | tf_op jit(solution)/shard_map/all_to_all | solution.py:138
  77.7 4.2 %collective-permute-start = (bf16[4,2,3,40,256]{4,3,2,1,0:T(8,128)(2,1)S(1)}, bf16[4,2,3,40,256]{4,3,2,1,0:T(8,128)(2,1)S(1)}, u32[]{:S(2)}, u32[]{:S(2)}) collective-permute-start(bf16[4,2,3,40,256]{4,3,2,1,0:T(8,128)(2,1)S(1)} %get-tuple-element.111), channel_id=1, source_target_pairs={{0,1},{1,0},{2,3},{3,2},{4,5},{5,4},{6,7},{7,6},{8,9},{9,8},{10,11... | collective-permute-start | bytes 1474568 | tf_op jit(solution)/shard_map/ppermute | solution.py:20
  79.3 12.1 %collective-permute-start.1 = (bf16[4,2,3,40,256]{4,3,2,1,0:T(8,128)(2,1)S(1)}, bf16[4,2,3,40,256]{4,3,2,1,0:T(8,128)(2,1)S(1)}, u32[]{:S(2)}, u32[]{:S(2)}) collective-permute-start(bf16[4,2,3,40,256]{4,3,2,1,0:T(8,128)(2,1)S(1)} %get-tuple-element.110), channel_id=1, source_target_pairs={{0,2},{1,3},{2,0},{3,1},{4,6},{5,7},{6,4},{7,5},{8,10},{9,11},{10,... | collective-permute-start | bytes 1474568 | tf_op jit(solution)/shard_map/ppermute | solution.py:20
  80.3 22.6 %collective-permute-start.2 = (bf16[4,2,3,40,256]{4,3,2,1,0:T(8,128)(2,1)S(1)}, bf16[4,2,3,40,256]{4,3,2,1,0:T(8,128)(2,1)S(1)}, u32[]{:S(2)}, u32[]{:S(2)}) collective-permute-start(bf16[4,2,3,40,256]{4,3,2,1,0:T(8,128)(2,1)S(1)} %get-tuple-element.109), channel_id=1, source_target_pairs={{0,3},{1,2},{2,1},{3,0},{4,7},{5,6},{6,5},{7,4},{8,11},{9,10},{10,... | collective-permute-start | bytes 1474568 | tf_op jit(solution)/shard_map/ppermute | solution.py:20
  111.2 20.2 %collective-permute-start.3 = (f32[1,3,256,256]{3,2,0,1:T(8,128)S(1)}, f32[1,3,256,256]{3,2,0,1:T(8,128)S(1)}, u32[]{:S(2)}, u32[]{:S(2)}) collective-permute-start(f32[1,3,256,256]{3,2,0,1:T(8,128)S(1)} %get-tuple-element.102), channel_id=1, source_target_pairs={{0,1},{1,2},{2,3},{3,4},{4,5},{5,6},{6,7},{7,8},{8,9},{9,10},{10,1... | collective-permute-start | bytes 2359304 | tf_op jit(solution)/shard_map/ppermute | solution.py:30
  114.0 18.6 %collective-permute-start.4 = (f32[1,3,256,256]{3,2,0,1:T(8,128)S(1)}, f32[1,3,256,256]{3,2,0,1:T(8,128)S(1)}, u32[]{:S(2)}, u32[]{:S(2)}) collective-permute-start(f32[1,3,256,256]{3,2,0,1:T(8,128)S(1)} %get-tuple-element.101), channel_id=1, source_target_pairs={{1,0},{2,1},{3,2},{4,3},{5,4},{6,5},{7,6},{8,7},{9,8},{10,9},{11,1... | collective-permute-start | bytes 2359304 | tf_op jit(solution)/shard_map/ppermute | solution.py:33
